TPU v7x, 32 devices: a whole 2x2x4 slice. The times are simulated.
32 devices in a mesh: seq: 8 (over z, y), head: 4 (over x, core).
Axes of the slice: x: 2, y: 2, z: 4, core: 2. Of those that a mesh axis runs over, the one named last changes fastest.
Arguments:
- queries: bfloat16 [1024, 12288], P('seq', 'head'), may hold values from -32 to 32
- keys: bfloat16 [1024, 768], P('seq', 'head'), may hold values from -4 to 4
- values: bfloat16 [1024, 512], P('seq', 'head'), may hold values from -6 to 6
- features: bfloat16 [1024, 2560], P('seq', 'head'), may hold values from -6 to 6
- positions: int32 [1024], P('seq'), may hold values from 0 to 767, as said below
- gate_weight: bfloat16 [2560, 128], replicated, may hold values from -0.125 to 0.125
- key_in: bfloat16 [4, 6144, 128], P('head'), may hold values from -0.078125 to 0.078125
- key_out: bfloat16 [4, 128, 192], P('head'), may hold values from -0.5 to 0.5
- value_in: bfloat16 [4, 4096, 128], P('head'), may hold values from -0.09375 to 0.09375
- value_out: bfloat16 [4, 128, 128], P('head'), may hold values from -0.5 to 0.5
Outputs:
- mixed: bfloat16 [1024, 8192], P('seq', 'head')
Inputs may be any that keep to these rules, and one draw needn't show every extreme that they name: positions rise by one from token to token and fall to 0 where one of at most three documents begins inside the slab; the first document began before or at the slab's first token and ends inside the slab.
All inputs are finite; a program needn't handle non-finite values.
Results may differ from a plain program's by a relative error of at most 0.0056.
Values may be sent and summed in bfloat16 or wider, within the bound.
No kernel may reach another device: no remote copies, remote signals or barrier semaphores. Data moves between devices by JAX's collectives and lax.ppermute only.
A program may use at most 64 MiB of HBM per device.

v0:
```python
import jax
import jax.numpy as jnp
from jax import lax
from jax.sharding import PartitionSpec as P

QH = 16
DK = 192
DV = 128
STRIDE = 16
BLOCK = 32
WINDOW = 512


NEG = -1e30


def from_behind(value, axis, by):
    length = lax.axis_size(axis)
    pairs = [(i, i + by) for i in range(length) if 0 <= i + by < length]
    return lax.ppermute(value, axis, pairs)


def contract(left, right):
    return lax.dot_general(
        left, right, (((1,), (1,)), ((), ())), preferred_element_type=jnp.float32
    )


def spread_rows(visible, heads):
    count, width = visible.shape
    return jnp.broadcast_to(visible[:, None, :], (count, heads, width)).reshape(
        count * heads, width
    )


def attend(rows, keys_used, values_used, visible):
    scores = contract(rows, keys_used) * DK ** (-0.5)
    top = jnp.max(jnp.where(visible, scores, NEG), axis=1, keepdims=True)
    weights = jnp.where(visible, jnp.exp(scores - top), 0.0)
    total = jnp.sum(weights, axis=1, keepdims=True)
    summed = jnp.dot(weights.astype(jnp.bfloat16), values_used, preferred_element_type=jnp.float32)
    return summed / jnp.maximum(total, 1.0)


def compress(rows, tail, weight_in, weight_out):
    width = rows.shape[1]
    halves = jnp.concatenate([rows, tail], 0).reshape(-1, STRIDE * width)
    split = STRIDE * width
    pre = jnp.dot(halves[:-1], weight_in[:split], preferred_element_type=jnp.float32)
    pre = pre + jnp.dot(halves[1:], weight_in[split:], preferred_element_type=jnp.float32)
    hidden = jax.nn.gelu(pre).astype(jnp.bfloat16)
    return jnp.dot(hidden, weight_out, preferred_element_type=jnp.float32).astype(jnp.bfloat16)


def code_seen(code_ids, token_ids, doc_start):
    first = STRIDE * code_ids
    return (first[None, :] + BLOCK - 1 <= token_ids[:, None]) & (
        first[None, :] >= doc_start[:, None]
    )


def on_device(
    queries, keys, values, features, positions, gate_weight, key_in, key_out, value_in, value_out
):
    count = keys.shape[0]
    here = lax.axis_index("seq")
    group = lax.axis_index("head")
    token_ids = here * count + jnp.arange(count, dtype=jnp.int32)
    doc_start = token_ids - positions
    whole = lax.all_gather(features, "head", axis=1, tiled=True)
    columns = lax.dynamic_slice_in_dim(gate_weight, group * (2 * QH), 2 * QH, 1)
    logits = jnp.dot(whole, columns, preferred_element_type=jnp.float32)
    tail_keys, tail_values = from_behind((keys[:STRIDE], values[:STRIDE]), "seq", -1)
    code_keys = compress(keys, tail_keys, key_in[0], key_out[0])
    code_values = compress(values, tail_values, value_in[0], value_out[0])
    rows = queries.reshape(count * QH, DK)
    all_keys, all_values = (
        lax.all_gather(code_keys, "seq", axis=0, tiled=True),
        lax.all_gather(code_values, "seq", axis=0, tiled=True),
    )
    code_ids = jnp.arange(all_keys.shape[0], dtype=jnp.int32)
    coarse = attend(
        rows, all_keys, all_values, spread_rows(code_seen(code_ids, token_ids, doc_start), QH)
    )
    reach = WINDOW // count
    earlier = []
    current = (keys, values)
    for step in range(reach):
        current = from_behind((current[0], current[1]), "seq", 1)
        earlier.insert(0, current)
    near_keys = jnp.concatenate([pair[0] for pair in earlier] + [keys], 0)
    near_values = jnp.concatenate([pair[1] for pair in earlier] + [values], 0)
    key_ids = (here - reach) * count + jnp.arange((reach + 1) * count, dtype=jnp.int32)
    near = (key_ids[None, :] >= 0) & (key_ids[None, :] <= token_ids[:, None])
    near = (
        near
        & (key_ids[None, :] > token_ids[:, None] - WINDOW)
        & (key_ids[None, :] >= doc_start[:, None])
    )
    local = attend(rows, near_keys, near_values, spread_rows(near, QH))
    gates = jax.nn.sigmoid(logits)
    mixed = gates[:, :QH, None] * coarse.reshape(count, QH, DV) + gates[
        :, QH:, None
    ] * local.reshape(count, QH, DV)
    return mixed.reshape(count, QH * DV).astype(jnp.bfloat16)


def solution(mesh):
    return jax.shard_map(
        on_device,
        mesh=mesh,
        in_specs=(
            P("seq", "head"),
            P("seq", "head"),
            P("seq", "head"),
            P("seq", "head"),
            P("seq"),
            P(),
            P("head", None, None),
            P("head", None, None),
            P("head", None, None),
            P("head", None, None),
        ),
        out_specs=P("seq", "head"),
        check_vma=False,
    )
```

profile of v0, /device:TPU:0, one launch (start us, length us, event | category | flops | bytes accessed | tf_op | source)
XLA Modules:
  0.0 135.7 jit_solution(18427063321453065143)
XLA Ops:
  0.0 5.0 %collective-permute-start.6 = (bf16[128,128]{1,0:T(8,128)(2,1)}, bf16[128,128]{1,0:T(8,128)(2,1)S(1)}, u32[]{:S(2)}, u32[]{:S(2)}) collective-permute-start(bf16[128,128]{1,0:T(8,128)(2,1)} %param.12), channel_id=1, source_target_pairs={{0,4},{4,8},{8,12},{12,16},{16,20},{20,24},{24,28},{1,5},{5,9},{9,... | collective-permute-start | bytes 98312 | tf_op jit(solution)/shard_map/ppermute | solution.py:20
  7.0 4.6 %collective-permute-start.2 = (bf16[128,192]{0,1:T(8,128)(2,1)}, bf16[128,192]{0,1:T(8,128)(2,1)S(1)}, u32[]{:S(2)}, u32[]{:S(2)}) collective-permute-start(bf16[128,192]{0,1:T(8,128)(2,1)} %param.11), channel_id=1, source_target_pairs={{0,4},{4,8},{8,12},{12,16},{16,20},{20,24},{24,28},{1,5},{5,9},{9,... | collective-permute-start | bytes 147464 | tf_op jit(solution)/shard_map/ppermute | solution.py:20
  11.6 1.3 collective-permute-start
  15.3 8.2 %all_gather.9 = bf16[128,2560]{1,0:T(8,128)(2,1)S(1)} all-gather(bf16[128,640]{1,0:T(8,128)(2,1)} %param.13), channel_id=1, replica_groups=mesh['seq'=8,'head'=4] {'head'}, dimensions={1}, use_global_device_ids=true | all-gather | bytes 819200 | tf_op jit(solution)/shard_map/all_gather | solution.py:70
  24.8 1.4 fusion.18
  27.0 5.0 %collective-permute-start.7 = (bf16[128,128]{1,0:T(8,128)(2,1)S(1)}, bf16[128,128]{1,0:T(8,128)(2,1)S(1)}, u32[]{:S(2)}, u32[]{:S(2)}) collective-permute-start(bf16[128,128]{1,0:T(8,128)(2,1)S(1)} %collective-permute-done.6), channel_id=1, source_target_pairs={{0,4},{4,8},{8,12},{12,16},{16,20},{20,24},{24,28},{1,5},{5,9},{9,... | collective-permute-start | bytes 98312 | tf_op jit(solution)/shard_map/ppermute | solution.py:20
  32.0 1.6 %collective-permute-done.7 = bf16[128,128]{1,0:T(8,128)(2,1)S(1)} collective-permute-done((bf16[128,128]{1,0:T(8,128)(2,1)S(1)}, bf16[128,128]{1,0:T(8,128)(2,1)S(1)}, u32[]{:S(2)}, u32[]{:S(2)}) %collective-permute-start.7) | collective-permute-done | bytes 32800 | tf_op jit(solution)/shard_map/ppermute | solution.py:20
  33.6 5.4 %collective-permute-start.8 = (bf16[128,128]{1,0:T(8,128)(2,1)S(1)}, bf16[128,128]{1,0:T(8,128)(2,1)}, u32[]{:S(2)}, u32[]{:S(2)}) collective-permute-start(bf16[128,128]{1,0:T(8,128)(2,1)S(1)} %collective-permute-done.7), channel_id=1, source_target_pairs={{0,4},{4,8},{8,12},{12,16},{16,20},{20,24},{24,28},{1,5},{5,9},{9,... | collective-permute-start | bytes 98312 | tf_op jit(solution)/shard_map/ppermute | solution.py:20
  39.0 4.5 %collective-permute-start.3 = (bf16[128,192]{0,1:T(8,128)(2,1)S(1)}, bf16[128,192]{0,1:T(8,128)(2,1)S(1)}, u32[]{:S(2)}, u32[]{:S(2)}) collective-permute-start(bf16[128,192]{0,1:T(8,128)(2,1)S(1)} %collective-permute-done.2), channel_id=1, source_target_pairs={{0,4},{4,8},{8,12},{12,16},{16,20},{20,24},{24,28},{1,5},{5,9},{9,... | collective-permute-start | bytes 147464 | tf_op jit(solution)/shard_map/ppermute | solution.py:20
  43.6 2.5 %collective-permute-start.9 = (bf16[128,128]{1,0:T(8,128)(2,1)}, bf16[128,128]{1,0:T(8,128)(2,1)}, u32[]{:S(2)}, u32[]{:S(2)}) collective-permute-start(bf16[128,128]{1,0:T(8,128)(2,1)} %collective-permute-done.8), channel_id=1, source_target_pairs={{0,4},{4,8},{8,12},{12,16},{16,20},{20,24},{24,28},{1,5},{5,9},{9,... | collective-permute-start | bytes 98312 | tf_op jit(solution)/shard_map/ppermute | solution.py:20
  46.6 1.4 %copy.20 = pred[2048,640]{0,1:T(32,128)(4,1)S(1)} copy(pred[2048,640]{1,0:T(8,128)(4,1)S(1)} %bitcast.76) | data formatting | bytes 2621440 | tf_op jit(solution)/shard_map/reshape | solution.py:31
  48.0 2.2 %reshape.196 = bf16[2048,192]{1,0:T(8,128)(2,1)S(1)} reshape(bf16[128,3072]{1,0:T(8,128)(2,1)} %param.10) | data formatting | bytes 1572864 | tf_op jit(solution)/shard_map/reshape | solution.py:76
  50.9 4.4 %collective-permute-start.4 = (bf16[128,192]{0,1:T(8,128)(2,1)S(1)}, bf16[128,192]{0,1:T(8,128)(2,1)S(1)}, u32[]{:S(2)}, u32[]{:S(2)}) collective-permute-start(bf16[128,192]{0,1:T(8,128)(2,1)S(1)} %collective-permute-done.3), channel_id=1, source_target_pairs={{0,4},{4,8},{8,12},{12,16},{16,20},{20,24},{24,28},{1,5},{5,9},{9,... | collective-permute-start | bytes 147464 | tf_op jit(solution)/shard_map/ppermute | solution.py:20
  58.3 3.5 %collective-permute-start.5 = (bf16[128,192]{0,1:T(8,128)(2,1)S(1)}, bf16[128,192]{0,1:T(8,128)(2,1)}, u32[]{:S(2)}, u32[]{:S(2)}) collective-permute-start(bf16[128,192]{0,1:T(8,128)(2,1)S(1)} %collective-permute-done.4), channel_id=1, source_target_pairs={{0,4},{4,8},{8,12},{12,16},{16,20},{20,24},{24,28},{1,5},{5,9},{9,... | collective-permute-start | bytes 147464 | tf_op jit(solution)/shard_map/ppermute | solution.py:20
  61.9 1.3 convolution_convert_fusion.1
  63.2 26.1 %all_gather.11 = bf16[64,128]{1,0:T(8,128)(2,1)S(1)} all-gather(bf16[8,128]{1,0:T(8,128)(2,1)S(1)} %convolution_convert_fusion.1), channel_id=1, replica_groups=mesh['seq'=8,'head'=4] {'seq'}, dimensions={0}, use_global_device_ids=true | all-gather | bytes 18432 | tf_op jit(solution)/shard_map/all_gather | solution.py:79
  92.4 1.4 %fusion.3 = f32[2048]{0:T(1024)S(1)} fusion(pred[2048,640]{0,1:T(32,128)(4,1)S(1)} %copy.20, f32[640,2048]{1,0:T(8,128)S(1)} %get-tuple-element.12, f32[2048]{0:T(1024)S(1)} %get-tuple-element.11), kind=kLoop, calls=%fused_computation.5 | loop fusion | flops 5240832 | bytes 6569984 | tf_op jit(solution)/shard_map/reduce_sum | solution.py:40
  93.8 2.6 %fusion.8 = f32[2048,128]{1,0:T(8,128)} fusion(bf16[640,128]{1,0:T(8,128)(2,1)S(1)} %copy-done.6, pred[2048,640]{0,1:T(32,128)(4,1)S(1)} %copy.20, f32[640,2048]{1,0:T(8,128)S(1)} %get-tuple-element.12, f32[2048]{0:T(1024)S(1)} %get-tuple-element.11, f32[2048]{0:T(1024)S(1)} %broadcast_maximum_fusion), kind=kOutput, calls=%fused_computation.11 | convolution fusion | flops 341049344 | bytes 7782400 | tf_op jit(solution)/shard_map/dot_general | solution.py:41
  96.4 1.4 %reshape.199 = f32[128,2048]{1,0:T(8,128)S(1)} reshape(f32[2048,128]{1,0:T(8,128)} %fusion.8) | data formatting | bytes 2097152 | tf_op jit(solution)/shard_map/reshape | solution.py:104
  98.0 1.5 %convolution_convert_fusion = bf16[8,192]{1,0:T(8,128)(2,1)S(1)} fusion(bf16[1,128,192]{1,2,0:T(8,128)(2,1)S(1)} %copy-done.3, f32[8,128]{1,0:T(8,128)S(1)} %fusion.18, bf16[8,3072]{1,0:T(8,128)(2,1)S(1)} %slice.62, bf16[1,6144,128]{2,1,0:T(8,128)(2,1)} %param.16), kind=kOutput, calls=%fused_computation.17 | convolution fusion | flops 6696448 | bytes 891904 | tf_op jit(solution)/shard_map/dot_general | solution.py:52
  99.5 30.6 %all_gather.10 = bf16[64,192]{1,0:T(8,128)(2,1)S(1)} all-gather(bf16[8,192]{1,0:T(8,128)(2,1)S(1)} %convolution_convert_fusion), channel_id=1, replica_groups=mesh['seq'=8,'head'=4] {'seq'}, dimensions={0}, use_global_device_ids=true | all-gather | bytes 27648 | tf_op jit(solution)/shard_map/all_gather | solution.py:78
  130.7 1.5 %convolution_divide_fusion = f32[2048,128]{1,0:T(8,128)} fusion(bf16[64,128]{1,0:T(8,128)(2,1)S(1)} %all_gather.11, f32[2048]{0:T(1024)S(1)} %broadcast_maximum_fusion.1, pred[2048,64]{0,1:T(32,128)(4,1)S(1)} %copy.17, f32[2048,64]{0,1:T(8,128)S(1)} %get-tuple-element.14, f32[2048]{0:T(1024)S(1)} %get-tuple-element.13), kind=kOutput, calls=%fused_computation.8 | convolution fusion | flops 34209792 | bytes 1736704 | tf_op jit(solution)/shard_map/dot_general | solution.py:41
  132.2 1.4 %reshape.197 = f32[128,2048]{1,0:T(8,128)S(1)} reshape(f32[2048,128]{1,0:T(8,128)} %convolution_divide_fusion) | data formatting | bytes 2097152 | tf_op jit(solution)/shard_map/reshape | solution.py:102
  134.2 1.5 %fusion.16 = bf16[128,2048]{1,0:T(8,128)(2,1)} fusion(f32[128,2048]{1,0:T(8,128)S(1)} %reshape.199, f32[16,8,16,128]{3,2,1,0:T(8,128)S(1)} %bitcast.77, f32[128,2048]{1,0:T(8,128)S(1)} %reshape.197, f32[16,8,16,128]{3,2,1,0:T(8,128)S(1)} %bitcast.78), kind=kLoop, calls=%fused_computation.23 | loop fusion | flops 1048576 | bytes 4718592 | tf_op jit(solution)/shard_map/convert_element_type | solution.py:105
  (63 shorter events, 15.1 us)
Async XLA Ops:
  0.0 26.2 %copy-start = (bf16[2560,128]{1,0:T(8,128)(2,1)S(1)}, bf16[2560,128]{1,0:T(8,128)(2,1)}, u32[]{:S(2)}) copy-start(bf16[2560,128]{1,0:T(8,128)(2,1)} %param.15) | copy-start | bytes 1966084
  0.0 27.0 %collective-permute-start.6 = (bf16[128,128]{1,0:T(8,128)(2,1)}, bf16[128,128]{1,0:T(8,128)(2,1)S(1)}, u32[]{:S(2)}, u32[]{:S(2)}) collective-permute-start(bf16[128,128]{1,0:T(8,128)(2,1)} %param.12), channel_id=1, source_target_pairs={{0,4},{4,8},{8,12},{12,16},{16,20},{20,24},{24,28},{1,5},{5,9},{9,... | collective-permute-start | bytes 98312 | tf_op jit(solution)/shard_map/ppermute | solution.py:20
  5.7 51.9 %collective-permute-start.1 = (bf16[16,128]{1,0:T(8,128)(2,1)S(1)}, bf16[16,128]{1,0:T(8,128)(2,1)S(1)}, u32[]{:S(2)}, u32[]{:S(2)}) collective-permute-start(bf16[16,128]{1,0:T(8,128)(2,1)S(1)} %slice.68), channel_id=1, source_target_pairs={{4,0},{8,4},{12,8},{16,12},{20,16},{24,20},{28,24},{5,1},{9,5},{13... | collective-permute-start | bytes 12296 | tf_op jit(solution)/shard_map/ppermute | solution.py:20
  7.0 32.0 %collective-permute-start.2 = (bf16[128,192]{0,1:T(8,128)(2,1)}, bf16[128,192]{0,1:T(8,128)(2,1)S(1)}, u32[]{:S(2)}, u32[]{:S(2)}) collective-permute-start(bf16[128,192]{0,1:T(8,128)(2,1)} %param.11), channel_id=1, source_target_pairs={{0,4},{4,8},{8,12},{12,16},{16,20},{20,24},{24,28},{1,5},{5,9},{9,... | collective-permute-start | bytes 147464 | tf_op jit(solution)/shard_map/ppermute | solution.py:20
  11.6 78.6 %collective-permute-start = (bf16[16,192]{0,1:T(8,128)(2,1)}, bf16[16,192]{0,1:T(8,128)(2,1)}, u32[]{:S(2)}, u32[]{:S(2)}) collective-permute-start(bf16[16,192]{0,1:T(8,128)(2,1)} %bitcast.80), channel_id=1, source_target_pairs={{4,0},{8,4},{12,8},{16,12},{20,16},{24,20},{28,24},{5,1},{9,5},{13... | collective-permute-start | bytes 18440 | tf_op jit(solution)/shard_map/ppermute | solution.py:20
  15.3 42.3 %copy-start.2 = (bf16[128,128]{1,0:T(8,128)(2,1)S(1)}, bf16[128,128]{1,0:T(8,128)(2,1)}, u32[]{:S(2)}) copy-start(bf16[128,128]{1,0:T(8,128)(2,1)} %param.12) | copy-start | bytes 98308
  24.8 65.4 %copy-start.1 = (bf16[128,192]{0,1:T(8,128)(2,1)S(1)}, bf16[128,192]{0,1:T(8,128)(2,1)}, u32[]{:S(2)}) copy-start(bf16[128,192]{0,1:T(8,128)(2,1)} %param.11) | copy-start | bytes 147460
  27.0 6.5 %collective-permute-start.7 = (bf16[128,128]{1,0:T(8,128)(2,1)S(1)}, bf16[128,128]{1,0:T(8,128)(2,1)S(1)}, u32[]{:S(2)}, u32[]{:S(2)}) collective-permute-start(bf16[128,128]{1,0:T(8,128)(2,1)S(1)} %collective-permute-done.6), channel_id=1, source_target_pairs={{0,4},{4,8},{8,12},{12,16},{16,20},{20,24},{24,28},{1,5},{5,9},{9,... | collective-permute-start | bytes 98312 | tf_op jit(solution)/shard_map/ppermute | solution.py:20
  33.6 13.0 %copy-start.4 = (bf16[128,128]{1,0:T(8,128)(2,1)}, bf16[128,128]{1,0:T(8,128)(2,1)S(1)}, u32[]{:S(2)}) copy-start(bf16[128,128]{1,0:T(8,128)(2,1)S(1)} %collective-permute-done.7) | copy-start | bytes 98308
  33.6 10.0 %collective-permute-start.8 = (bf16[128,128]{1,0:T(8,128)(2,1)S(1)}, bf16[128,128]{1,0:T(8,128)(2,1)}, u32[]{:S(2)}, u32[]{:S(2)}) collective-permute-start(bf16[128,128]{1,0:T(8,128)(2,1)S(1)} %collective-permute-done.7), channel_id=1, source_target_pairs={{0,4},{4,8},{8,12},{12,16},{16,20},{20,24},{24,28},{1,5},{5,9},{9,... | collective-permute-start | bytes 98312 | tf_op jit(solution)/shard_map/ppermute | solution.py:20
  39.0 11.9 %collective-permute-start.3 = (bf16[128,192]{0,1:T(8,128)(2,1)S(1)}, bf16[128,192]{0,1:T(8,128)(2,1)S(1)}, u32[]{:S(2)}, u32[]{:S(2)}) collective-permute-start(bf16[128,192]{0,1:T(8,128)(2,1)S(1)} %collective-permute-done.2), channel_id=1, source_target_pairs={{0,4},{4,8},{8,12},{12,16},{16,20},{20,24},{24,28},{1,5},{5,9},{9,... | collective-permute-start | bytes 147464 | tf_op jit(solution)/shard_map/ppermute | solution.py:20
  43.6 11.7 %collective-permute-start.9 = (bf16[128,128]{1,0:T(8,128)(2,1)}, bf16[128,128]{1,0:T(8,128)(2,1)}, u32[]{:S(2)}, u32[]{:S(2)}) collective-permute-start(bf16[128,128]{1,0:T(8,128)(2,1)} %collective-permute-done.8), channel_id=1, source_target_pairs={{0,4},{4,8},{8,12},{12,16},{16,20},{20,24},{24,28},{1,5},{5,9},{9,... | collective-permute-start | bytes 98312 | tf_op jit(solution)/shard_map/ppermute | solution.py:20
  50.9 7.5 %collective-permute-start.4 = (bf16[128,192]{0,1:T(8,128)(2,1)S(1)}, bf16[128,192]{0,1:T(8,128)(2,1)S(1)}, u32[]{:S(2)}, u32[]{:S(2)}) collective-permute-start(bf16[128,192]{0,1:T(8,128)(2,1)S(1)} %collective-permute-done.3), channel_id=1, source_target_pairs={{0,4},{4,8},{8,12},{12,16},{16,20},{20,24},{24,28},{1,5},{5,9},{9,... | collective-permute-start | bytes 147464 | tf_op jit(solution)/shard_map/ppermute | solution.py:20
  57.6 0.7 copy-start.5
  58.3 31.0 %collective-permute-start.5 = (bf16[128,192]{0,1:T(8,128)(2,1)S(1)}, bf16[128,192]{0,1:T(8,128)(2,1)}, u32[]{:S(2)}, u32[]{:S(2)}) collective-permute-start(bf16[128,192]{0,1:T(8,128)(2,1)S(1)} %collective-permute-done.4), channel_id=1, source_target_pairs={{0,4},{4,8},{8,12},{12,16},{16,20},{20,24},{24,28},{1,5},{5,9},{9,... | collective-permute-start | bytes 147464 | tf_op jit(solution)/shard_map/ppermute | solution.py:20
  92.4 1.4 %copy-start.6 = (bf16[640,128]{1,0:T(8,128)(2,1)S(1)}, bf16[640,128]{1,0:T(8,128)(2,1)}, u32[]{:S(2)}) copy-start(bf16[640,128]{1,0:T(8,128)(2,1)} %copy-done.5) | copy-start | bytes 491524
  93.8 4.2 %copy-start.3 = (bf16[1,128,192]{1,2,0:T(8,128)(2,1)S(1)}, bf16[1,128,192]{1,2,0:T(8,128)(2,1)}, u32[]{:S(2)}) copy-start(bf16[1,128,192]{1,2,0:T(8,128)(2,1)} %param.17) | copy-start | bytes 147460
where the time goes:
time: 137 us; the launch traced here: 136 us
  blocking collectives  65 us (47%)
  starting transfers between devices  37.5 us (27%)
  local copies, waits for them, and re-layouts  14.6 us (11%)
  matrix products  11.7 us (9%)
  other arithmetic  4.91 us (4%)
  waiting for transfers between devices  1.59 us (1%)
    ppermute x10, starting transfers between devices, from_behind(): return lax.ppermute(value, axis, pairs)  37.5 us
    all_gather x1, blocking collectives, on_device(): lax.all_gather(code_keys, 'seq', axis=0, tiled=True)  30.6 us
    all_gather x1, blocking collectives, on_device(): lax.all_gather(code_values, 'seq', axis=0, tiled=True)  26.1 us
    all_gather x1, blocking collectives, on_device(): whole = lax.all_gather(features, 'head', axis=1, tiled=True)  8.21 us
    unnamed x23, local copies, waits for them, and re-layouts  4.75 us
    dot_general x2, matrix products, attend(): jnp.dot(weights.astype(jnp.bfloat16), values_used, preferred_element_type...  4.04 us
    dot_general x2, matrix products, compress(): jnp.dot(hidden, weight_out, preferred_element_type=jnp.float32)  2.8 us
  transfers between devices with their start and end apart: 10, of which 1 were waited for; matrix products, arithmetic and copies ran while one was open for 12% of the time, Pallas kernels for 0%

commit v1 on v0

v1 whole, which is shorter than its diff:
```python
import functools

import jax
import jax.numpy as jnp
from jax import lax
from jax.experimental import pallas as pl
from jax.experimental.pallas import tpu as pltpu
from jax.sharding import PartitionSpec as P

QH = 16
DK = 192
DV = 128
STRIDE = 16
BLOCK = 32
WINDOW = 512
LANES = 128
PAD = 256
GROUP = 4

NEG = -1e30
SCALE = DK ** (-0.5) * 1.4426950408889634

f32 = jnp.float32
bf16 = jnp.bfloat16


def up(value, step):
    return -(-value // step) * step


def swap(value, axis, by):
    length = lax.axis_size(axis)
    return lax.ppermute(value, axis, [(i, i ^ by) for i in range(length)])


def turn(value, axis, by):
    length = lax.axis_size(axis)
    return lax.ppermute(value, axis, [(i, (i + by) % length) for i in range(length)])


def dot(left, right):
    return jnp.dot(left, right, preferred_element_type=f32)


def dot_t(left, right):
    return lax.dot_general(left, right, (((1,), (1,)), ((), ())), preferred_element_type=f32)


def logit_kernel(head, features, columns, *outs_and_scratch):
    outs, total = outs_and_scratch[:-1], outs_and_scratch[-1]
    total[...] = lax.dot_general(
        columns[...], features[...], (((0,), (1,)), ((), ())), preferred_element_type=f32
    )
    for step, out in enumerate(outs):
        first = (head[0] ^ step if len(outs) & (len(outs) - 1) == 0 else (head[0] + step) % len(outs)) * (2 * QH)
        out[...] = total[pl.ds(pl.multiple_of(first, 2 * QH), 2 * QH), :]


def gate_logits(features, gate_weight, group, heads):
    count, depth = features.shape
    part = jax.ShapeDtypeStruct((2 * QH, count), f32)
    parts = pl.pallas_call(
        logit_kernel,
        grid_spec=pltpu.PrefetchScalarGridSpec(
            num_scalar_prefetch=1,
            grid=(1,),
            in_specs=[
                pl.BlockSpec((count, depth), lambda i, head: (0, 0)),
                pl.BlockSpec((depth, gate_weight.shape[1]), lambda i, head: (head[0], 0)),
            ],
            out_specs=[pl.BlockSpec((2 * QH, count), lambda i, head: (0, 0))] * heads,
            scratch_shapes=[pltpu.VMEM((gate_weight.shape[1], count), f32)],
        ),
        out_shape=[part] * heads,
        name="gate_logits",
    )(group[None], features, gate_weight)
    if heads & (heads - 1) == 0:
        return [parts[0]] + [swap(parts[d], "head", d) for d in range(1, heads)]
    return [parts[0]] + [turn(parts[d], "head", d) for d in range(1, heads)]


def gelu(x):
    return 0.5 * x * (1.0 + jnp.tanh(0.7978845608028654 * (x + 0.044715 * x * x * x)))


def halves(rows, planes, size, weight, width):
    strides = size // STRIDE
    total = jnp.zeros((strides, 2 * LANES), f32)
    for place in range(STRIDE):
        part = jnp.concatenate(
            [rows[pl.ds(plane * size + place, strides, stride=STRIDE), :] for plane in planes], 1
        ).astype(bf16)[:, :width]
        both = jnp.concatenate(
            [
                weight[pl.ds(place * width, width), :],
                weight[pl.ds((STRIDE + place) * width, width), :],
            ],
            1,
        )
        total = total + dot(part, both)
    return total[:, :LANES], total[:, LANES:]


def hidden_of(first, second):
    strides = first.shape[0]
    later = pltpu.roll(second, strides - 1, axis=0)
    last = lax.broadcasted_iota(jnp.int32, later.shape, 0) == strides - 1
    return gelu(first + jnp.where(last, 0.0, later)).astype(bf16)


def unpack(block, rows, size, at):
    count = block.shape[1]
    for plane in range(2):
        part = block[plane * LANES : min((plane + 1) * LANES, DK), :].astype(f32).T
        rows[pl.ds(plane * size + at, count), : part.shape[1]] = part
    rows[pl.ds(2 * size + at, count), :] = block[DK:, :].astype(f32)


def codes_of(rows, size, key_in, key_out, value_in, value_out):
    key_hidden = hidden_of(*halves(rows, (0, 1), size, key_in, DK))
    code_keys = dot_t(key_out[...], key_hidden).astype(bf16)
    value_hidden = hidden_of(*halves(rows, (2,), size, value_in, DV))
    code_values = dot(value_hidden, value_out[...]).astype(bf16)
    return code_keys, code_values


def attend_body(
    here, count, reach, get_block, code_keys, code_values, codes, positions, q, parts, out, scratch
):
    even, odd, near_values, far_values, near_bias, far_bias, gates = scratch
    near = (reach + 1) * count
    far = even.shape[1] - near
    lengths = jnp.broadcast_to(positions[...].astype(f32), (count, count)).T.astype(jnp.int32)

    def lens(width):
        return jnp.concatenate([lengths] * (width // count), 1) if width > count else lengths

    def ids(width, axis):
        return lax.broadcasted_iota(jnp.int32, (count, width), axis)

    token = here * count + ids(near, 0)
    key = (here - reach) * count + ids(near, 1)
    seen = (key <= token) & (key > token - WINDOW) & (key >= token - lens(near)) & (key >= 0)
    near_bias[...] = jnp.where(seen, 0.0, NEG)
    token = here * count + ids(far, 0)
    first = STRIDE * ids(far, 1)
    seen = (first + (BLOCK - 1) <= token) & (first >= token - lens(far)) & (ids(far, 1) < codes)
    far_bias[...] = jnp.where(seen, 0.0, NEG)
    some = jnp.max(jnp.where(seen, 1.0, 0.0), axis=1, keepdims=True)

    total = parts[0][...]
    for part in parts[1:]:
        total = total + part[...]
    total = jax.nn.sigmoid(total)
    total = jnp.concatenate([total, jnp.zeros((LANES - 2 * QH, count), f32)], 0).T
    coarse_lane = lax.broadcasted_iota(jnp.int32, total.shape, 1) < QH
    gates[...] = jnp.where(coarse_lane, total * some, total)

    even[DK:, :] = jnp.zeros((PAD - DK, near + far), bf16)
    odd[: PAD - DK, :] = jnp.zeros((PAD - DK, near + far), bf16)
    near_values[:, DV:] = jnp.ones((near, DV), bf16)
    far_values[:, DV:] = jnp.ones((far, DV), bf16)
    for step in range(reach + 1):
        block = get_block(jnp.maximum(here - reach + step, 0), step)
        lanes = slice(step * count, (step + 1) * count)
        even[:DK, lanes] = block[:DK, :]
        odd[PAD - DK :, lanes] = block[:DK, :]
        near_values[lanes, :DV] = block[DK:, :]
    even[:DK, near:] = code_keys
    odd[PAD - DK :, near:] = code_keys
    far_values[:, :DV] = code_values

    pair = 2 * DK
    for side in (0, 1):
        keys = (even, odd)[side]
        for chunk in range(0, QH // 2, GROUP):
            rows = jnp.concatenate(
                [
                    q[:, (chunk + j) * pair + side * LANES : (chunk + j) * pair + side * LANES + PAD]
                    for j in range(GROUP)
                ],
                0,
            )
            scores = dot(rows, keys[...])

            def branch(scores, bias, values):
                width = scores.shape[1]
                scores = scores.reshape(GROUP, count, width) + bias[...][None]
                top = jnp.max(scores, axis=2, keepdims=True)
                weights = jnp.exp2((scores - top) * SCALE).astype(bf16)
                summed = dot(weights.reshape(GROUP * count, width), values[...])
                return summed[:, :DV] / jnp.maximum(summed[:, DV:], 1.0)

            local = branch(scores[:, :near], near_bias, near_values)
            coarse = branch(scores[:, near:], far_bias, far_values)
            for j in range(GROUP):
                head = 2 * (chunk + j) + side
                at = slice(j * count, (j + 1) * count)
                mixed = (
                    gates[:, head : head + 1] * coarse[at]
                    + gates[:, QH + head : QH + head + 1] * local[at]
                )
                out[:, head * DV : (head + 1) * DV] = mixed.astype(bf16)


def attend_scratch(count, reach, far):
    near = (reach + 1) * count
    return [
        pltpu.VMEM((PAD, near + far), bf16),
        pltpu.VMEM((PAD, near + far), bf16),
        pltpu.VMEM((near, 2 * DV), bf16),
        pltpu.VMEM((far, 2 * DV), bf16),
        pltpu.VMEM((count, near), f32),
        pltpu.VMEM((count, far), f32),
        pltpu.VMEM((count, LANES), f32),
    ]


def whole_kernel(slots, heads, count, reach, here_ref, *refs):
    positions, q_hbm = refs[:2]
    blocks = refs[2 : 2 + slots]
    weights = refs[2 + slots : 6 + slots]
    parts = refs[6 + slots : 6 + slots + heads]
    out = refs[6 + slots + heads]
    q, held, key_in, key_out, value_in, value_out, rows, sems = refs[
        7 + slots + heads : 15 + slots + heads
    ]
    scratch = refs[15 + slots + heads :]
    here = here_ref[0]
    copies = [
        pltpu.make_async_copy(block, held.at[here ^ d], sems.at[d]) for d, block in enumerate(blocks)
    ]
    places = (key_in, key_out, value_in, value_out)
    copies += [
        pltpu.make_async_copy(source, place, sems.at[slots + i])
        for i, (source, place) in enumerate(zip(weights, places))
    ]
    copies.append(pltpu.make_async_copy(q_hbm, q, sems.at[slots + 4]))
    for copy in copies:
        copy.start()
    for copy in copies[:slots]:
        copy.wait()
    for slot in range(slots):
        unpack(held[slot], rows, slots * count, slot * count)
    for copy in copies[slots:]:
        copy.wait()
    codes = slots * count // STRIDE
    far = up(codes, LANES)
    code_keys, code_values = codes_of(rows, slots * count, key_in, key_out, value_in, value_out)
    if far > codes:
        code_keys = jnp.concatenate([code_keys, jnp.zeros((DK, far - codes), bf16)], 1)
        code_values = jnp.concatenate([code_values, jnp.zeros((far - codes, DV), bf16)], 0)
    attend_body(
        here, count, reach, lambda at, step: held[at], code_keys, code_values, codes,
        positions, q, parts, out, scratch,
    )


def whole_slab(here, positions, queries, blocks, weights, parts, reach):
    count = queries.shape[0]
    slots, heads = len(blocks), len(parts)
    far = up(slots * count // STRIDE, LANES)
    anywhere = pl.BlockSpec(memory_space=pl.ANY)
    vmem = pl.BlockSpec(memory_space=pltpu.VMEM)
    return pl.pallas_call(
        functools.partial(whole_kernel, slots, heads, count, reach),
        in_specs=[pl.BlockSpec(memory_space=pltpu.SMEM), vmem]
        + [anywhere] * (1 + slots + 4)
        + [vmem] * heads,
        out_specs=vmem,
        out_shape=jax.ShapeDtypeStruct((count, QH * DV), bf16),
        scratch_shapes=[
            pltpu.VMEM(queries.shape, bf16),
            pltpu.VMEM((slots, DK + DV, count), bf16),
        ]
        + [pltpu.VMEM(w.shape, bf16) for w in weights]
        + [
            pltpu.VMEM((3 * slots * count, LANES), f32),
            pltpu.SemaphoreType.DMA((slots + 5,)),
        ]
        + attend_scratch(count, reach, far),
        name="whole_slab",
    )(here[None], positions[None, :], queries, *blocks, *weights, *parts)


def codes_kernel(before, block, key_in, key_out, value_in, value_out, out, rows):
    count = block.shape[1]
    unpack(before[...], rows, 2 * count, 0)
    unpack(block[...], rows, 2 * count, count)
    code_keys, code_values = codes_of(rows, 2 * count, key_in, key_out, value_in, value_out)
    out[:, :DK] = code_keys.astype(f32).T
    out[:, DK:] = code_values.astype(f32)


def near_kernel(heads, count, reach, codes, here_ref, *refs):
    positions, q = refs[:2]
    blocks = refs[2 : 3 + reach]
    code_keys, code_values = refs[3 + reach : 5 + reach]
    parts = refs[5 + reach : 5 + reach + heads]
    out = refs[5 + reach + heads]
    attend_body(
        here_ref[0], count, reach, lambda at, step: blocks[step][...], code_keys[...], code_values[...],
        codes, positions, q, parts, out, refs[6 + reach + heads :],
    )


def long_slab(here, positions, queries, block, weights, parts, reach, length):
    count = queries.shape[0]
    strides = count // STRIDE
    smem, vmem = pl.BlockSpec(memory_space=pltpu.SMEM), pl.BlockSpec(memory_space=pltpu.VMEM)
    earlier = [turn(block, "seq", reach - k) for k in range(reach)]
    made = pl.pallas_call(
        codes_kernel,
        in_specs=[vmem] * 6,
        out_specs=vmem,
        out_shape=jax.ShapeDtypeStruct((2 * strides, DK + DV), f32),
        scratch_shapes=[pltpu.VMEM((6 * count, LANES), f32)],
        name="codes",
    )(earlier[-1], block, *weights)
    mine = made[strides - 1 : 2 * strides - 1].astype(bf16)
    every = lax.all_gather(mine, "seq", axis=0, tiled=True)[1:]
    codes = length * count // STRIDE
    far = up(codes, LANES)
    every = jnp.concatenate([every, jnp.zeros((far - every.shape[0], DK + DV), bf16)], 0)
    return pl.pallas_call(
        functools.partial(near_kernel, len(parts), count, reach, codes),
        in_specs=[smem] + [vmem] * (5 + reach + len(parts)),
        out_specs=vmem,
        out_shape=jax.ShapeDtypeStruct((count, QH * DV), bf16),
        scratch_shapes=attend_scratch(count, reach, far),
        name="long_slab",
    )(here[None], positions[None, :], queries, *earlier, block, every[:, :DK].T, every[:, DK:], *parts)


def on_device(
    queries, keys, values, features, positions, gate_weight, key_in, key_out, value_in, value_out
):
    count = keys.shape[0]
    length, heads = lax.axis_size("seq"), lax.axis_size("head")
    here = lax.axis_index("seq")
    group = lax.axis_index("head")
    reach = -(-WINDOW // count)
    block = jnp.concatenate([keys.T, values], 0)
    weights = (key_in[0], key_out[0].T, value_in[0], value_out[0])
    if length != 8:
        parts = gate_logits(features, gate_weight, group, heads)
        return long_slab(here, positions, queries, block, weights, parts, reach, length)
    slots = {0: block, 1: swap(block, "seq", 1)}
    for d in (2, 4, 6):
        slots[d] = swap(block, "seq", d)
    for d in (2, 4, 6):
        slots[d + 1] = swap(slots[d], "seq", 1)
    parts = gate_logits(features, gate_weight, group, heads)
    blocks = [slots[d] for d in range(length)]
    return whole_slab(here, positions, queries, blocks, weights, parts, reach)


def solution(mesh):
    return jax.shard_map(
        on_device,
        mesh=mesh,
        in_specs=(
            P("seq", "head"),
            P("seq", "head"),
            P("seq", "head"),
            P("seq", "head"),
            P("seq"),
            P(),
            P("head", None, None),
            P("head", None, None),
            P("head", None, None),
            P("head", None, None),
        ),
        out_specs=P("seq", "head"),
        check_vma=False,
    )
```

time: 137 us -> 34.5 us (0.25)
  blocking collectives: 65 us -> 0 us
  starting transfers between devices: 37.5 us -> 12.9 us
  local copies, waits for them, and re-layouts: 14.6 us -> 0.64 us
  matrix products: 11.7 us -> 0 us
  Pallas kernels: 0 us -> 9.8 us
  waiting for transfers between devices: 1.59 us -> 9.99 us
  other arithmetic: 4.91 us -> 0.82 us
    all_gather x3 -> x0, blocking collectives: 65 us -> none  [the longest x1 30.6 us: on_device(): lax.all_gather(code_keys, 'seq', axis=0, tiled=True)]
    ppermute x10, starting transfers between devices: 37.5 us -> 12.9 us  [swap(): return lax.ppermute(value, axis, [(i, i ^ by) for i in range(length)])]
    dot_general x9 -> x0, matrix products: 11.7 us -> none  [the longest x2 4.04 us: attend(): jnp.dot(weights.astype(jnp.bfloat16), values_used, preferred_element_type...]
    pallas_call x0 -> x2, Pallas kernels: none -> 9.8 us  [the longest x1 7.94 us: whole_slab(): pl.pallas_call(functools.partial(whole_kernel, slots, heads, count, reach...]
    ppermute x10, waiting for transfers between devices: 1.59 us -> 9.99 us  [swap(): return lax.ppermute(value, axis, [(i, i ^ by) for i in range(length)])]
    reshape x5 -> x0, local copies, waits for them, and re-layouts: 6.78 us -> none  [the longest x1 2.24 us: on_device(): rows = queries.reshape(count * QH, DK)]
    unnamed x23 -> x22, local copies, waits for them, and re-layouts: 4.75 us -> 0.64 us
    slice x9 -> x0, local copies, waits for them, and re-layouts: 2.04 us -> none  [the longest x2 0.89 us: compress(): halves[:-1]]
  transfers between devices with their start and end apart: 10 -> 10, of which waited for: 1 -> 5; matrix products, arithmetic and copies ran while one was open for 12% -> 0% of each run, Pallas kernels for 0% -> 5%
where the time goes in v1:
time: 34.5 us; the launch traced here: 34.3 us
  starting transfers between devices  12.9 us (37%)
  waiting for transfers between devices  9.99 us (29%)
  Pallas kernels  9.8 us (28%)
  other arithmetic  0.82 us (2%)
  local copies, waits for them, and re-layouts  0.64 us (2%)
    ppermute x10, starting transfers between devices, swap(): return lax.ppermute(value, axis, [(i, i ^ by) for i in range(length)])  12.9 us
    ppermute x10, waiting for transfers between devices, swap(): return lax.ppermute(value, axis, [(i, i ^ by) for i in range(length)])  9.99 us
    pallas_call x1, Pallas kernels, whole_slab(): pl.pallas_call(functools.partial(whole_kernel, slots, heads, count, reach...  7.94 us
    pallas_call x1, Pallas kernels, gate_logits(): pl.pallas_call(logit_kernel, grid_spec=pltpu.PrefetchScalarGridSpec(num_s...  1.86 us
    concatenate x1, other arithmetic, on_device(): block = jnp.concatenate([keys.T, values], 0)  0.82 us
  transfers between devices with their start and end apart: 10, of which 5 were waited for; matrix products, arithmetic and copies ran while one was open for 0% of the time, Pallas kernels for 5%

profile of v1, /device:TPU:0, one launch (start us, length us, event | category | flops | bytes accessed | tf_op | source)
XLA Modules:
  0.0 34.3 jit_solution(2410272749509101802)
XLA Ops:
  0.0 0.8 %pad_maximum_fusion.refs_2_ = bf16[320,128]{1,0:T(8,128)(2,1)S(1)} fusion(bf16[128,128]{1,0:T(8,128)(2,1)} %param.12, bf16[192,128]{1,0:T(8,128)(2,1)} %bitcast.12), kind=kLoop, calls=%fused_computation | loop fusion | flops 163840 | bytes 163840 | tf_op jit(solution)/shard_map/concatenate | solution.py:343
  0.8 5.1 %collective-permute-start.5 = (bf16[320,128]{1,0:T(8,128)(2,1)S(1)}, bf16[320,128]{1,0:T(8,128)(2,1)S(1)}, u32[]{:S(2)}, u32[]{:S(2)}) collective-permute-start(bf16[320,128]{1,0:T(8,128)(2,1)S(1)} %pad_maximum_fusion.refs_2_), channel_id=1, source_target_pairs={{0,24},{4,28},{8,16},{12,20},{16,8},{20,12},{24,0},{28,4},{1,25},{... | collective-permute-start | bytes 245768 | tf_op jit(solution)/shard_map/ppermute | solution.py:33
  6.0 0.0 collective-permute-start.3
  6.0 0.6 %collective-permute-start.1 = (bf16[320,128]{1,0:T(8,128)(2,1)S(1)}, bf16[320,128]{1,0:T(8,128)(2,1)S(1)}, u32[]{:S(2)}, u32[]{:S(2)}) collective-permute-start(bf16[320,128]{1,0:T(8,128)(2,1)S(1)} %pad_maximum_fusion.refs_2_), channel_id=1, source_target_pairs={{0,8},{4,12},{8,0},{12,4},{16,24},{20,28},{24,16},{28,20},{1,9},{5... | collective-permute-start | bytes 245768 | tf_op jit(solution)/shard_map/ppermute | solution.py:33
  6.6 1.7 %collective-permute-start = (bf16[320,128]{1,0:T(8,128)(2,1)S(1)}, bf16[320,128]{1,0:T(8,128)(2,1)S(1)}, u32[]{:S(2)}, u32[]{:S(2)}) collective-permute-start(bf16[320,128]{1,0:T(8,128)(2,1)S(1)} %pad_maximum_fusion.refs_2_), channel_id=1, source_target_pairs={{0,4},{4,0},{8,12},{12,8},{16,20},{20,16},{24,28},{28,24},{1,5},{5... | collective-permute-start | bytes 245768 | tf_op jit(solution)/shard_map/ppermute | solution.py:33
  8.3 0.6 %collective-permute-done.5.refs_8_ = bf16[320,128]{1,0:T(8,128)(2,1)S(1)} collective-permute-done((bf16[320,128]{1,0:T(8,128)(2,1)S(1)}, bf16[320,128]{1,0:T(8,128)(2,1)S(1)}, u32[]{:S(2)}, u32[]{:S(2)}) %collective-permute-start.5) | collective-permute-done | bytes 81952 | tf_op jit(solution)/shard_map/ppermute | solution.py:33
  8.9 1.8 %collective-permute-start.6 = (bf16[320,128]{1,0:T(8,128)(2,1)S(1)}, bf16[320,128]{1,0:T(8,128)(2,1)S(1)}, u32[]{:S(2)}, u32[]{:S(2)}) collective-permute-start(bf16[320,128]{1,0:T(8,128)(2,1)S(1)} %collective-permute-done.5.refs_8_), channel_id=1, source_target_pairs={{0,4},{4,0},{8,12},{12,8},{16,20},{20,16},{24,28},{28,24},{1,5},{5... | collective-permute-start | bytes 245768 | tf_op jit(solution)/shard_map/ppermute | solution.py:33
  10.7 2.1 %collective-permute-done.3.refs_6_ = bf16[320,128]{1,0:T(8,128)(2,1)S(1)} collective-permute-done((bf16[320,128]{1,0:T(8,128)(2,1)S(1)}, bf16[320,128]{1,0:T(8,128)(2,1)S(1)}, u32[]{:S(2)}, u32[]{:S(2)}) %collective-permute-start.3) | collective-permute-done | bytes 81952 | tf_op jit(solution)/shard_map/ppermute | solution.py:33
  12.8 1.5 %collective-permute-start.4 = (bf16[320,128]{1,0:T(8,128)(2,1)S(1)}, bf16[320,128]{1,0:T(8,128)(2,1)S(1)}, u32[]{:S(2)}, u32[]{:S(2)}) collective-permute-start(bf16[320,128]{1,0:T(8,128)(2,1)S(1)} %collective-permute-done.3.refs_6_), channel_id=1, source_target_pairs={{0,4},{4,0},{8,12},{12,8},{16,20},{20,16},{24,28},{28,24},{1,5},{5... | collective-permute-start | bytes 245768 | tf_op jit(solution)/shard_map/ppermute | solution.py:33
  14.3 0.0 collective-permute-done.1.refs_4_
  14.4 0.5 %collective-permute-start.2 = (bf16[320,128]{1,0:T(8,128)(2,1)S(1)}, bf16[320,128]{1,0:T(8,128)(2,1)S(1)}, u32[]{:S(2)}, u32[]{:S(2)}) collective-permute-start(bf16[320,128]{1,0:T(8,128)(2,1)S(1)} %collective-permute-done.1.refs_4_), channel_id=1, source_target_pairs={{0,4},{4,0},{8,12},{12,8},{16,20},{20,16},{24,28},{28,24},{1,5},{5... | collective-permute-start | bytes 245768 | tf_op jit(solution)/shard_map/ppermute | solution.py:33
  14.9 1.9 %gate_logits.1 = (f32[32,128]{1,0:T(8,128)}, f32[32,128]{1,0:T(8,128)}, f32[32,128]{1,0:T(8,128)}, f32[32,128]{1,0:T(8,128)}) custom-call(s32[1]{0:T(128)} %bitcast.8.head, bf16[128,640]{1,0:T(8,128)(2,1)} %features.1, bf16[2560,128]{1,0:T(8,128)(2,1)} %columns.1), custom_call_target="tpu_custom_call" | custom-call | tf_op jit(solution)/shard_map/gate_logits/pallas_call | solution.py:62
  16.7 1.4 %collective-permute-done.7.refs_15_ = f32[32,128]{1,0:T(8,128)S(1)} collective-permute-done((f32[32,128]{1,0:T(8,128)}, f32[32,128]{1,0:T(8,128)S(1)}, u32[]{:S(2)}, u32[]{:S(2)}) %collective-permute-start.7) | collective-permute-done | bytes 16416 | tf_op jit(solution)/shard_map/ppermute | solution.py:33
  18.1 1.5 %collective-permute-start.8 = (f32[32,128]{1,0:T(8,128)}, f32[32,128]{1,0:T(8,128)S(1)}, u32[]{:S(2)}, u32[]{:S(2)}) collective-permute-start(f32[32,128]{1,0:T(8,128)} %get-tuple-element.11), channel_id=1, source_target_pairs={{0,2},{1,3},{2,0},{3,1},{4,6},{5,7},{6,4},{7,5},{8,10},{9,11},{10,... | collective-permute-start | bytes 49160 | tf_op jit(solution)/shard_map/ppermute | solution.py:33
  19.6 2.5 %collective-permute-done.8.refs_16_ = f32[32,128]{1,0:T(8,128)S(1)} collective-permute-done((f32[32,128]{1,0:T(8,128)}, f32[32,128]{1,0:T(8,128)S(1)}, u32[]{:S(2)}, u32[]{:S(2)}) %collective-permute-start.8) | collective-permute-done | bytes 16416 | tf_op jit(solution)/shard_map/ppermute | solution.py:33
  22.1 0.1 collective-permute-start.9
  22.2 3.4 %collective-permute-done.9.refs_17_ = f32[32,128]{1,0:T(8,128)S(1)} collective-permute-done((f32[32,128]{1,0:T(8,128)}, f32[32,128]{1,0:T(8,128)S(1)}, u32[]{:S(2)}, u32[]{:S(2)}) %collective-permute-start.9) | collective-permute-done | bytes 16416 | tf_op jit(solution)/shard_map/ppermute | solution.py:33
  25.6 0.0 collective-permute-done.4.refs_7_
  25.7 0.5 %copy-done.10 = f32[32,128]{1,0:T(8,128)} copy-done((f32[32,128]{1,0:T(8,128)}, f32[32,128]{1,0:T(8,128)S(1)}, u32[]{:S(2)}) %copy-start.10) | copy-done | bytes 16408
  26.2 0.0 copy-done.4
  26.2 0.0 copy-done.5
  26.2 0.0 copy-done.6
  26.3 0.0 copy-done.7
  26.3 7.9 %whole_slab.1 = bf16[128,2048]{1,0:T(8,128)(2,1)} custom-call(s32[1]{0:T(128)} %bitcast.here_ref, s32[1,128]{1,0:T(1,128)} %bitcast.15, bf16[128,3072]{1,0:T(8,128)(2,1)} %refs_1_.1, bf16[320,128]{1,0:T(8,128)(2,1)} %copy-done, bf16[320,128]{1,0:T(8,128)(2,1)} %copy-done.4, bf16[320,128]{1,0:T(8,128)(2,1)} %copy-done.3, bf16[320,128]{1,0:T(8,128)(2,1)} %copy-done.7, ...), custom_call_target="tpu_custom_call" | custom-call | tf_op jit(solution)/shard_map/whole_slab/pallas_call | solution.py:265
  (21 shorter events, 0.0 us)
Async XLA Ops:
  0.8 24.8 %copy-start = (bf16[320,128]{1,0:T(8,128)(2,1)}, bf16[320,128]{1,0:T(8,128)(2,1)S(1)}, u32[]{:S(2)}) copy-start(bf16[320,128]{1,0:T(8,128)(2,1)S(1)} %pad_maximum_fusion.refs_2_) | copy-start | bytes 245764
  0.8 8.1 %collective-permute-start.5 = (bf16[320,128]{1,0:T(8,128)(2,1)S(1)}, bf16[320,128]{1,0:T(8,128)(2,1)S(1)}, u32[]{:S(2)}, u32[]{:S(2)}) collective-permute-start(bf16[320,128]{1,0:T(8,128)(2,1)S(1)} %pad_maximum_fusion.refs_2_), channel_id=1, source_target_pairs={{0,24},{4,28},{8,16},{12,20},{16,8},{20,12},{24,0},{28,4},{1,25},{... | collective-permute-start | bytes 245768 | tf_op jit(solution)/shard_map/ppermute | solution.py:33
  6.0 6.9 %collective-permute-start.3 = (bf16[320,128]{1,0:T(8,128)(2,1)S(1)}, bf16[320,128]{1,0:T(8,128)(2,1)S(1)}, u32[]{:S(2)}, u32[]{:S(2)}) collective-permute-start(bf16[320,128]{1,0:T(8,128)(2,1)S(1)} %pad_maximum_fusion.refs_2_), channel_id=1, source_target_pairs={{0,16},{4,20},{8,24},{12,28},{16,0},{20,4},{24,8},{28,12},{1,17},{... | collective-permute-start | bytes 245768 | tf_op jit(solution)/shard_map/ppermute | solution.py:33
  6.0 8.4 %collective-permute-start.1 = (bf16[320,128]{1,0:T(8,128)(2,1)S(1)}, bf16[320,128]{1,0:T(8,128)(2,1)S(1)}, u32[]{:S(2)}, u32[]{:S(2)}) collective-permute-start(bf16[320,128]{1,0:T(8,128)(2,1)S(1)} %pad_maximum_fusion.refs_2_), channel_id=1, source_target_pairs={{0,8},{4,12},{8,0},{12,4},{16,24},{20,28},{24,16},{28,20},{1,9},{5... | collective-permute-start | bytes 245768 | tf_op jit(solution)/shard_map/ppermute | solution.py:33
  6.6 19.0 %collective-permute-start = (bf16[320,128]{1,0:T(8,128)(2,1)S(1)}, bf16[320,128]{1,0:T(8,128)(2,1)S(1)}, u32[]{:S(2)}, u32[]{:S(2)}) collective-permute-start(bf16[320,128]{1,0:T(8,128)(2,1)S(1)} %pad_maximum_fusion.refs_2_), channel_id=1, source_target_pairs={{0,4},{4,0},{8,12},{12,8},{16,20},{20,16},{24,28},{28,24},{1,5},{5... | collective-permute-start | bytes 245768 | tf_op jit(solution)/shard_map/ppermute | solution.py:33
  8.9 16.7 %copy-start.1 = (bf16[320,128]{1,0:T(8,128)(2,1)}, bf16[320,128]{1,0:T(8,128)(2,1)S(1)}, u32[]{:S(2)}) copy-start(bf16[320,128]{1,0:T(8,128)(2,1)S(1)} %collective-permute-done.5.refs_8_) | copy-start | bytes 245764
  8.9 16.7 %collective-permute-start.6 = (bf16[320,128]{1,0:T(8,128)(2,1)S(1)}, bf16[320,128]{1,0:T(8,128)(2,1)S(1)}, u32[]{:S(2)}, u32[]{:S(2)}) collective-permute-start(bf16[320,128]{1,0:T(8,128)(2,1)S(1)} %collective-permute-done.5.refs_8_), channel_id=1, source_target_pairs={{0,4},{4,0},{8,12},{12,8},{16,20},{20,16},{24,28},{28,24},{1,5},{5... | collective-permute-start | bytes 245768 | tf_op jit(solution)/shard_map/ppermute | solution.py:33
  12.8 12.8 %copy-start.2 = (bf16[320,128]{1,0:T(8,128)(2,1)}, bf16[320,128]{1,0:T(8,128)(2,1)S(1)}, u32[]{:S(2)}) copy-start(bf16[320,128]{1,0:T(8,128)(2,1)S(1)} %collective-permute-done.3.refs_6_) | copy-start | bytes 245764
  12.8 12.8 %collective-permute-start.4 = (bf16[320,128]{1,0:T(8,128)(2,1)S(1)}, bf16[320,128]{1,0:T(8,128)(2,1)S(1)}, u32[]{:S(2)}, u32[]{:S(2)}) collective-permute-start(bf16[320,128]{1,0:T(8,128)(2,1)S(1)} %collective-permute-done.3.refs_6_), channel_id=1, source_target_pairs={{0,4},{4,0},{8,12},{12,8},{16,20},{20,16},{24,28},{28,24},{1,5},{5... | collective-permute-start | bytes 245768 | tf_op jit(solution)/shard_map/ppermute | solution.py:33
  14.4 11.3 %copy-start.3 = (bf16[320,128]{1,0:T(8,128)(2,1)}, bf16[320,128]{1,0:T(8,128)(2,1)S(1)}, u32[]{:S(2)}) copy-start(bf16[320,128]{1,0:T(8,128)(2,1)S(1)} %collective-permute-done.1.refs_4_) | copy-start | bytes 245764
  14.4 11.3 %collective-permute-start.2 = (bf16[320,128]{1,0:T(8,128)(2,1)S(1)}, bf16[320,128]{1,0:T(8,128)(2,1)S(1)}, u32[]{:S(2)}, u32[]{:S(2)}) collective-permute-start(bf16[320,128]{1,0:T(8,128)(2,1)S(1)} %collective-permute-done.1.refs_4_), channel_id=1, source_target_pairs={{0,4},{4,0},{8,12},{12,8},{16,20},{20,16},{24,28},{28,24},{1,5},{5... | collective-permute-start | bytes 245768 | tf_op jit(solution)/shard_map/ppermute | solution.py:33
  16.7 1.4 %collective-permute-start.7 = (f32[32,128]{1,0:T(8,128)}, f32[32,128]{1,0:T(8,128)S(1)}, u32[]{:S(2)}, u32[]{:S(2)}) collective-permute-start(f32[32,128]{1,0:T(8,128)} %get-tuple-element.10), channel_id=1, source_target_pairs={{0,1},{1,0},{2,3},{3,2},{4,5},{5,4},{6,7},{7,6},{8,9},{9,8},{10,11... | collective-permute-start | bytes 49160 | tf_op jit(solution)/shard_map/ppermute | solution.py:33
  18.1 7.6 %copy-start.8 = (f32[32,128]{1,0:T(8,128)}, f32[32,128]{1,0:T(8,128)S(1)}, u32[]{:S(2)}) copy-start(f32[32,128]{1,0:T(8,128)S(1)} %collective-permute-done.7.refs_15_) | copy-start | bytes 49156
  18.1 3.9 %collective-permute-start.8 = (f32[32,128]{1,0:T(8,128)}, f32[32,128]{1,0:T(8,128)S(1)}, u32[]{:S(2)}, u32[]{:S(2)}) collective-permute-start(f32[32,128]{1,0:T(8,128)} %get-tuple-element.11), channel_id=1, source_target_pairs={{0,2},{1,3},{2,0},{3,1},{4,6},{5,7},{6,4},{7,5},{8,10},{9,11},{10,... | collective-permute-start | bytes 49160 | tf_op jit(solution)/shard_map/ppermute | solution.py:33
  22.1 3.6 %copy-start.9 = (f32[32,128]{1,0:T(8,128)}, f32[32,128]{1,0:T(8,128)S(1)}, u32[]{:S(2)}) copy-start(f32[32,128]{1,0:T(8,128)S(1)} %collective-permute-done.8.refs_16_) | copy-start | bytes 49156
  22.1 3.5 %collective-permute-start.9 = (f32[32,128]{1,0:T(8,128)}, f32[32,128]{1,0:T(8,128)S(1)}, u32[]{:S(2)}, u32[]{:S(2)}) collective-permute-start(f32[32,128]{1,0:T(8,128)} %get-tuple-element.12), channel_id=1, source_target_pairs={{0,3},{1,2},{2,1},{3,0},{4,7},{5,6},{6,5},{7,4},{8,11},{9,10},{10,... | collective-permute-start | bytes 49160 | tf_op jit(solution)/shard_map/ppermute | solution.py:33
  25.6 0.6 %copy-start.10 = (f32[32,128]{1,0:T(8,128)}, f32[32,128]{1,0:T(8,128)S(1)}, u32[]{:S(2)}) copy-start(f32[32,128]{1,0:T(8,128)S(1)} %collective-permute-done.9.refs_17_) | copy-start | bytes 49156
  25.6 0.6 %copy-start.4 = (bf16[320,128]{1,0:T(8,128)(2,1)}, bf16[320,128]{1,0:T(8,128)(2,1)S(1)}, u32[]{:S(2)}) copy-start(bf16[320,128]{1,0:T(8,128)(2,1)S(1)} %collective-permute-done.refs_3_) | copy-start | bytes 245764
  25.6 0.7 %copy-start.5 = (bf16[320,128]{1,0:T(8,128)(2,1)}, bf16[320,128]{1,0:T(8,128)(2,1)S(1)}, u32[]{:S(2)}) copy-start(bf16[320,128]{1,0:T(8,128)(2,1)S(1)} %collective-permute-done.6.refs_9_) | copy-start | bytes 245764
  25.6 0.7 %copy-start.6 = (bf16[320,128]{1,0:T(8,128)(2,1)}, bf16[320,128]{1,0:T(8,128)(2,1)S(1)}, u32[]{:S(2)}) copy-start(bf16[320,128]{1,0:T(8,128)(2,1)S(1)} %collective-permute-done.4.refs_7_) | copy-start | bytes 245764
  25.6 0.7 %copy-start.7 = (bf16[320,128]{1,0:T(8,128)(2,1)}, bf16[320,128]{1,0:T(8,128)(2,1)S(1)}, u32[]{:S(2)}) copy-start(bf16[320,128]{1,0:T(8,128)(2,1)S(1)} %collective-permute-done.2.refs_5_) | copy-start | bytes 245764
